TPU v7x, 32 devices: a whole 2x2x4 slice. The times are simulated.
32 devices in a mesh: gx: 8 (over y, x, core), gy: 4 (over z).
Axes of the slice: x: 2, y: 2, z: 4, core: 2. Of those that a mesh axis runs over, the one named last changes fastest.
Arguments:
- fields: float32 [5, 128, 128, 128], P(None, 'gx', 'gy'), may hold values from -6 to 6
- patch_weight: bfloat16 [2560, 512], replicated, may hold values from -0.125 to 0.125
- trainer_of: int32 [2048, 1], P(('gx', 'gy')), may hold values from 0 to 31; in each aligned block of 64 rows (0 to 63, 64 to 127, ...) at most 4 rows name the same one
- lag_index: int32 [16, 16, 16], P('gx', 'gy'), may hold values from 0 to 1
- w_in: bfloat16 [32, 512, 2048], P(('gx', 'gy')), may hold values from -0.25 to 0.25
- b_in: float32 [32, 2048], P(('gx', 'gy')), may hold values from -3 to 3
- w_out: bfloat16 [32, 2048, 512], P(('gx', 'gy')), may hold values from -0.125 to 0.125
- b_out: float32 [32, 512], P(('gx', 'gy')), may hold values from -3 to 3
Outputs:
- new_fields: float32 [5, 128, 128, 128], P(None, 'gx', 'gy')
- patch_gradient: float32 [2560, 512], replicated
- w_in_gradient: float32 [32, 512, 2048], P(('gx', 'gy'))
- b_in_gradient: float32 [32, 2048], P(('gx', 'gy'))
- w_out_gradient: float32 [32, 2048, 512], P(('gx', 'gy'))
- b_out_gradient: float32 [32, 512], P(('gx', 'gy'))
Inputs may be any that keep to these rules, and one draw needn't show every extreme that they name: `trainer_of`: among the 64 rows of one brick, no trainer is named more than 4 times.
All inputs are finite; a program needn't handle non-finite values.
Results may differ from a plain program's by a relative error of at most 0.0062.
Values may be sent and summed in bfloat16 or wider, within the bound.
A program may use at most 128 MiB of HBM per device.

v0:
```python
import jax
import jax.numpy as jnp
from jax import lax
from jax.sharding import PartitionSpec as P

FIELDS = 5
PATCH = 8
STEPS = 3
EMBED = 512
BLOCK_ROWS = 2
time_step = 0.2
viscosity = 0.5
drift_x = 0.6
drift_y = -0.4
drift_z = 0.3
error_weight = 0.0625


def with_halo(cells, sides, width):
    for axis, dim in sides:
        count = lax.axis_size(axis)
        ends = count - 1
        head = lax.slice_in_dim(cells, 0, width, axis=dim)
        tail = lax.slice_in_dim(cells, cells.shape[dim] - width, cells.shape[dim], axis=dim)
        cells = jnp.concatenate(
            [
                lax.ppermute(tail, axis, [(i, (i + 1) % count) for i in range(ends)]),
                cells,
                lax.ppermute(head, axis, [((i + 1) % count, i) for i in range(ends)]),
            ],
            axis=dim,
        )
    return cells


def shifted(padded, dimension, offset):
    window = [slice(None)]
    for other in (1, 2, 3):
        window.append(slice(2, padded.shape[other] - 2))
    window[dimension] = slice(2 + offset, padded.shape[dimension] - 2 + offset)
    return padded[tuple(window)]


def tendency(padded):
    gradients = []
    laplacian = 0.0
    for dimension in (1, 2, 3):
        back_two = shifted(padded, dimension, -2)
        back_one = shifted(padded, dimension, -1)
        middle = shifted(padded, dimension, 0)
        ahead_one = shifted(padded, dimension, 1)
        ahead_two = shifted(padded, dimension, 2)
        gradients.append((back_two - 8.0 * back_one + 8.0 * ahead_one - ahead_two) / 12.0)
        laplacian = (
            laplacian
            + (-back_two + 16.0 * back_one - 30.0 * middle + 16.0 * ahead_one - ahead_two) / 12.0
        )
    carried = drift_x * gradients[0] + drift_y * gradients[1] + drift_z * gradients[2]
    divergence = gradients[0][1] + gradients[1][2] + gradients[2][3]
    acoustic = jnp.stack(
        [divergence, gradients[0][4], gradients[1][4], gradients[2][4], divergence]
    )
    return viscosity * laplacian - carried - acoustic


def contract_rows(left, right):
    return lax.dot_general(
        left, right, (((0,), (0,)), ((), ())), preferred_element_type=jnp.float32
    )


def contract_cols(left, right):
    return lax.dot_general(
        left, right, (((1,), (1,)), ((), ())), preferred_element_type=jnp.float32
    )


def trainer_step(source, target, valid, w_first, b_first, w_second, b_second):
    pre = jnp.dot(source, w_first, preferred_element_type=jnp.float32) + b_first
    hidden = jax.nn.silu(pre).astype(jnp.bfloat16)
    predict = jnp.dot(hidden, w_second, preferred_element_type=jnp.float32) + b_second
    error = (error_weight * (predict - target.astype(jnp.float32)) * valid).astype(jnp.bfloat16)
    b_second_grad = jnp.sum(error.astype(jnp.float32), axis=0)
    w_second_grad = contract_rows(hidden, error)
    back = contract_cols(error, w_second)
    sigma = jax.nn.sigmoid(pre)
    pre_grad = (back * sigma * (1.0 + pre * (1.0 - sigma))).astype(jnp.bfloat16)
    b_first_grad = jnp.sum(pre_grad.astype(jnp.float32), axis=0)
    w_first_grad = contract_rows(source, pre_grad)
    source_grad = contract_cols(pre_grad, w_first).astype(jnp.bfloat16)
    return (source_grad, w_first_grad, b_first_grad, w_second_grad, b_second_grad)


def patchify(state):
    width_x, width_y, width_z = (state.shape[1], state.shape[2], state.shape[3])
    shaped = state.reshape(
        FIELDS, width_x // PATCH, PATCH, width_y // PATCH, PATCH, width_z // PATCH, PATCH
    )
    return shaped.transpose(1, 3, 5, 0, 2, 4, 6).reshape(-1, FIELDS * PATCH**3)


def pad_third(current):
    return jnp.pad(current, ((0, 0), (0, 0), (0, 0), (2, 2)))


def advance(fields):
    states = []
    current = fields
    for counter in range(STEPS):
        padded = with_halo(current, (("gx", 1), ("gy", 2)), 2)
        current = current + time_step * tendency(pad_third(padded))
        states.append(current)
    return states


def per_device(fields, patch_weight, trainer_of, lag_index, w_in, b_in, w_out, b_out):
    states = advance(fields)
    devices = lax.axis_size("gx") * lax.axis_size("gy")
    lag_rows = lag_index.reshape(-1, 1)
    picked = patchify(states[0].astype(jnp.bfloat16))
    picked = jnp.where(lag_rows == 1, patchify(states[1].astype(jnp.bfloat16)), picked)
    target = jnp.dot(
        patchify(states[-1].astype(jnp.bfloat16)), patch_weight, preferred_element_type=jnp.float32
    ).astype(jnp.bfloat16)
    patch_count = picked.shape[0]
    block_count = patch_count // BLOCK_ROWS
    slot_count = max(2, 2 * block_count // devices)
    owners = trainer_of[:, 0]
    onehot = (owners[:, None] == jnp.arange(devices, dtype=jnp.int32)[None, :]).astype(jnp.int32)
    within_rank = jnp.sum((jnp.cumsum(onehot, axis=0) - onehot) * onehot, axis=1)
    block_slot = owners * slot_count + within_rank

    def into_slots(rows):
        width = rows.shape[1]
        blocks = rows.reshape(block_count, BLOCK_ROWS, width)
        buffer = (
            jnp.zeros((devices * slot_count, BLOCK_ROWS, width), rows.dtype)
            .at[block_slot]
            .set(blocks)
        )
        return buffer.reshape(devices, slot_count, BLOCK_ROWS, width)

    valid_send = jnp.zeros((devices * slot_count,), jnp.bfloat16).at[block_slot].set(1.0)
    valid_send = valid_send.reshape(devices, slot_count)
    got_patches, got_target, got_valid = (
        lax.all_to_all(into_slots(picked), ("gx", "gy"), split_axis=0, concat_axis=0, tiled=True),
        lax.all_to_all(into_slots(target), ("gx", "gy"), split_axis=0, concat_axis=0, tiled=True),
        lax.all_to_all(valid_send, ("gx", "gy"), split_axis=0, concat_axis=0, tiled=True),
    )
    flat_patches = got_patches.reshape(-1, FIELDS * PATCH**3)
    source = jnp.dot(flat_patches, patch_weight, preferred_element_type=jnp.float32).astype(
        jnp.bfloat16
    )
    valid_rows = jnp.repeat(got_valid.astype(jnp.float32).reshape(-1), BLOCK_ROWS)[:, None]
    results = trainer_step(
        source, got_target.reshape(-1, EMBED), valid_rows, w_in[0], b_in[0], w_out[0], b_out[0]
    )
    partial_value = contract_rows(flat_patches, results[0])
    patch_gradient = lax.psum(partial_value, ("gx", "gy"))
    return (
        states[-1],
        patch_gradient,
        results[1][None],
        results[2][None],
        results[3][None],
        results[4][None],
    )


def solution(mesh):
    in_specs = (
        P(None, "gx", "gy", None),
        P(),
        P(("gx", "gy"), None),
        P("gx", "gy", None),
        P(("gx", "gy"), None, None),
        P(("gx", "gy"), None),
        P(("gx", "gy"), None, None),
        P(("gx", "gy"), None),
    )
    out_specs = (
        P(None, "gx", "gy", None),
        P(),
        P(("gx", "gy"), None, None),
        P(("gx", "gy"), None),
        P(("gx", "gy"), None, None),
        P(("gx", "gy"), None),
    )
    return jax.shard_map(
        per_device, mesh=mesh, in_specs=in_specs, out_specs=out_specs, check_vma=False
    )
```

profile of v0, /device:TPU:0, one launch (start us, length us, event | category | flops | bytes accessed | tf_op | source)
XLA Modules:
  0.0 457.9 jit_solution(11400775036131845433)
XLA Ops:
  8.4 2.4 collective-permute-start
  10.8 1.3 collective-permute-start.1
  13.8 1.8 constant_dynamic-update-slice_fusion
  16.3 3.8 collective-permute-start.2
  20.1 1.3 collective-permute-start.3
  22.3 4.3 collective-permute-done.3
  26.6 1.6 select_maximum_fusion.8
  28.2 2.3 broadcast_multiply_fusion.2
  31.9 4.0 fusion.57
  37.0 4.0 collective-permute-start.4
  44.1 8.5 %all-to-all-start.2 = ((bf16[32,1,4]{2,1,0:T(2,128)(2,1)}), bf16[32,1,4]{2,1,0:T(2,128)(2,1)S(1)}, u32[]{:S(2)}, u32[]{:S(2)}) async-start(bf16[32,1,4]{2,1,0:T(2,128)(2,1)} %all_to_all.16), calls=%async_computation.2 | async-start | bytes 32768 | tf_op jit(solution)/shard_map/all_to_all | solution.py:148
  53.9 3.7 collective-permute-start.6
  57.5 1.6 collective-permute-start.7
  59.9 4.2 collective-permute-done.7
  64.1 3.5 select_maximum_fusion.4
  69.8 3.9 fusion.59
  74.8 1.3 collective-permute-start.8
  76.1 1.8 collective-permute-start.9
  78.6 14.4 %reshape.78 = bf16[5,2,8,4,8,16,8]{6,5,4,3,2,1,0:T(8,128)(2,1)} reshape(bf16[5,16,32,128]{3,2,1,0:T(8,128)(2,1)} %get-tuple-element.8) | data formatting | bytes 1310720 | tf_op jit(solution)/shard_map/reshape | solution.py:96
  93.1 10.7 %copy.18 = bf16[2,4,16,5,8,8,8]{6,5,4,3,2,1,0:T(8,128)(2,1)} copy(bf16[2,4,16,5,8,8,8]{6,2,5,1,4,0,3:T(8,128)(2,1)} %bitcast.69) | data formatting | bytes 1310720 | tf_op jit(solution)/shard_map/transpose | solution.py:99
  103.8 14.5 %reshape.79 = bf16[64,2,2560]{2,1,0:T(2,128)(2,1)} reshape(bf16[2,4,16,5,8,8,8]{6,5,4,3,2,1,0:T(8,128)(2,1)} %copy.18) | data formatting | bytes 1310720 | tf_op jit(solution)/shard_map/reshape | solution.py:99
  118.3 14.4 %reshape.76 = bf16[5,2,8,4,8,16,8]{6,5,4,3,2,1,0:T(8,128)(2,1)} reshape(bf16[5,16,32,128]{3,2,1,0:T(8,128)(2,1)} %get-tuple-element.10) | data formatting | bytes 1310720 | tf_op jit(solution)/shard_map/reshape | solution.py:96
  132.7 10.6 %copy.17 = bf16[2,4,16,5,8,8,8]{6,5,4,3,2,1,0:T(8,128)(2,1)} copy(bf16[2,4,16,5,8,8,8]{6,2,5,1,4,0,3:T(8,128)(2,1)} %bitcast.70) | data formatting | bytes 1310720 | tf_op jit(solution)/shard_map/transpose | solution.py:99
  143.3 14.5 %reshape.77 = bf16[64,2,2560]{2,1,0:T(2,128)(2,1)} reshape(bf16[2,4,16,5,8,8,8]{6,5,4,3,2,1,0:T(8,128)(2,1)} %copy.17) | data formatting | bytes 1310720 | tf_op jit(solution)/shard_map/reshape | solution.py:99
  159.1 3.4 collective-permute-start.10
  162.5 1.5 collective-permute-start.11
  164.7 4.3 collective-permute-done.11
  169.0 3.5 select_maximum_fusion
  174.8 4.1 fusion.55
  178.9 14.4 %reshape.82 = bf16[5,2,8,4,8,16,8]{6,5,4,3,2,1,0:T(8,128)(2,1)} reshape(bf16[5,16,32,128]{3,2,1,0:T(8,128)(2,1)} %get-tuple-element.6) | data formatting | bytes 1310720 | tf_op jit(solution)/shard_map/reshape | solution.py:96
  193.3 13.3 %copy.19 = bf16[2,4,16,5,8,8,8]{2,1,0,6,5,4,3:T(4,128)(2,1)} copy(bf16[2,4,16,5,8,8,8]{6,2,5,1,4,0,3:T(8,128)(2,1)} %bitcast.71) | data formatting | bytes 1310720 | tf_op jit(solution)/shard_map/transpose | solution.py:99
  206.6 7.3 %reshape.83 = bf16[128,2560]{0,1:T(8,128)(2,1)S(1)} reshape(bf16[2,4,16,5,8,8,8]{2,1,0,6,5,4,3:T(4,128)(2,1)} %copy.19) | data formatting | bytes 1310720 | tf_op jit(solution)/shard_map/reshape | solution.py:99
  215.4 7.8 %scatter_fusion.1 = bf16[128,2,512]{2,1,0:T(2,128)(2,1)} fusion(bf16[128,2,512]{2,1,0:T(2,128)(2,1)} %broadcast_in_dim.41, s32[64]{0:T(128)S(1)} %fusion.52, bf16[64,2,512]{2,1,0:T(2,128)(2,1)S(1)} %reshape.99), kind=kCustom, calls=%fused_computation.1 | custom fusion | bytes 393472 | tf_op jit(solution)/shard_map/scatter | solution.py:139
  223.3 6.9 %all-to-all-start.1 = ((bf16[32,4,2,512]{3,2,1,0:T(2,128)(2,1)}), bf16[32,4,2,512]{3,2,1,0:T(2,128)(2,1)S(1)}, u32[]{:S(2)}, u32[]{:S(2)}) async-start(bf16[32,4,2,512]{3,2,1,0:T(2,128)(2,1)} %bitcast.11), calls=%async_computation.1 | async-start | bytes 524288 | tf_op jit(solution)/shard_map/all_to_all | solution.py:147
  230.2 2.1 broadcast_select_fusion
  232.3 1.7 broadcast_in_dim.39
  234.0 8.2 %scatter_fusion = bf16[128,2,2560]{2,1,0:T(2,128)(2,1)} fusion(bf16[128,2,2560]{2,1,0:T(2,128)(2,1)} %broadcast_in_dim.39, s32[64]{0:T(128)} %copy-done.13, bf16[64,2,2560]{2,1,0:T(2,128)(2,1)S(1)} %broadcast_select_fusion), kind=kCustom, calls=%fused_computation | custom fusion | bytes 1966336 | tf_op jit(solution)/shard_map/scatter | solution.py:139
  242.2 6.1 %all-to-all-start = ((bf16[32,4,2,2560]{3,2,1,0:T(2,128)(2,1)}), bf16[32,4,2,2560]{3,2,1,0:T(2,128)(2,1)}, u32[]{:S(2)}, u32[]{:S(2)}) async-start(bf16[32,4,2,2560]{3,2,1,0:T(2,128)(2,1)} %bitcast.72), calls=%async_computation | async-start | bytes 2621440 | tf_op jit(solution)/shard_map/all_to_all | solution.py:146
  249.6 29.0 %all-to-all-done = bf16[32,4,2,2560]{3,2,1,0:T(2,128)(2,1)} async-done(((bf16[32,4,2,2560]{3,2,1,0:T(2,128)(2,1)}), bf16[32,4,2,2560]{3,2,1,0:T(2,128)(2,1)}, u32[]{:S(2)}, u32[]{:S(2)}) %all-to-all-start) | async-done | bytes 1310752 | tf_op jit(solution)/shard_map/all_to_all | solution.py:146
  278.7 4.1 reshape.81
  282.7 2.3 convolution_convert_fusion
  286.9 1.3 convert_reduce_fusion.1
  288.2 2.7 convert_reduce_fusion
  291.0 6.2 %fusion.46 = f32[2560,512]{1,0:T(8,128)} fusion(bf16[256,2560]{1,0:T(8,128)(2,1)} %reshape.81, bf16[256,2048]{1,0:T(8,128)(2,1)} %get-tuple-element.48, bf16[1,512,2048]{2,1,0:T(8,128)(2,1)} %param.12), kind=kOutput, calls=%fused_computation.96 | convolution fusion | flops 1208090624 | bytes 9699328 | tf_op jit(solution)/shard_map/dot_general | solution.py:67
  297.2 4.1 convolution_bitcast_fusion.1
  301.4 2.8 convolution_bitcast_fusion
  304.2 141.2 %all-reduce.5.cloned.1.call-done = f32[2560,512]{1,0:T(8,128)} async-done(((f32[2560,512]{1,0:T(8,128)}), f32[2560,512]{1,0:T(8,128)}) %all-reduce.5.cloned.1.call-update) | async-done | bytes 5242896 | tf_op jit(solution)/shard_map/psum | solution.py:159
  445.4 5.4 %copy.40 = f32[2560,512]{1,0:T(8,128)} copy(f32[2560,512]{1,0:T(8,128)} %all-reduce.5.cloned.1.call-done) | data formatting | bytes 10485760
  (96 shorter events, 24.6 us)
Async XLA Ops:
  7.2 206.8 %copy-start = (bf16[2560,512]{1,0:T(8,128)(2,1)S(1)}, bf16[2560,512]{1,0:T(8,128)(2,1)}, u32[]{:S(2)}) copy-start(bf16[2560,512]{1,0:T(8,128)(2,1)} %param.9) | copy-start | bytes 7864324
  8.4 5.4 %collective-permute-start = (f32[5,2,32,128]{3,2,1,0:T(8,128)S(1)}, f32[5,2,32,128]{3,2,1,0:T(8,128)S(1)}, u32[]{:S(2)}, u32[]{:S(2)}) collective-permute-start(f32[5,2,32,128]{3,2,1,0:T(8,128)S(1)} %get-tuple-element.42), channel_id=1, source_target_pairs={{0,4},{4,8},{8,12},{12,16},{16,20},{20,24},{24,28},{1,5},{5,9},{9,... | collective-permute-start | bytes 491528 | tf_op jit(solution)/shard_map/ppermute | solution.py:27
  10.8 5.4 %collective-permute-start.1 = (f32[5,2,32,128]{3,2,1,0:T(8,128)S(1)}, f32[5,2,32,128]{3,2,1,0:T(8,128)S(1)}, u32[]{:S(2)}, u32[]{:S(2)}) collective-permute-start(f32[5,2,32,128]{3,2,1,0:T(8,128)S(1)} %get-tuple-element.41), channel_id=1, source_target_pairs={{4,0},{8,4},{12,8},{16,12},{20,16},{24,20},{28,24},{5,1},{9,5},{13... | collective-permute-start | bytes 491528 | tf_op jit(solution)/shard_map/ppermute | solution.py:29
  16.3 6.0 %collective-permute-start.2 = (f32[5,20,2,128]{3,2,1,0:T(2,128)S(1)}, f32[5,20,2,128]{3,2,1,0:T(2,128)S(1)}, u32[]{:S(2)}, u32[]{:S(2)}) collective-permute-start(f32[5,20,2,128]{3,2,1,0:T(2,128)S(1)} %get-tuple-element.32), channel_id=1, source_target_pairs={{0,1},{1,2},{2,3},{4,5},{5,6},{6,7},{8,9},{9,10},{10,11},{12,13},{... | collective-permute-start | bytes 307208 | tf_op jit(solution)/shard_map/ppermute | solution.py:27
  20.1 6.6 %collective-permute-start.3 = (f32[5,20,2,128]{3,2,1,0:T(2,128)S(1)}, f32[5,20,2,128]{3,2,1,0:T(2,128)S(1)}, u32[]{:S(2)}, u32[]{:S(2)}) collective-permute-start(f32[5,20,2,128]{3,2,1,0:T(2,128)S(1)} %get-tuple-element.33), channel_id=1, source_target_pairs={{1,0},{2,1},{3,2},{5,4},{6,5},{7,6},{9,8},{10,9},{11,10},{13,12},{... | collective-permute-start | bytes 307208 | tf_op jit(solution)/shard_map/ppermute | solution.py:29
  30.6 1.3 copy-start.6
  31.9 10.4 %copy-start.12 = (s32[64,1]{0,1:T(1,128)S(1)}, s32[64,1]{0,1:T(1,128)}, u32[]{:S(2)}) copy-start(s32[64,1]{0,1:T(1,128)} %param.10) | copy-start | bytes 772
  35.9 1.1 copy-start.3
  37.0 15.6 %collective-permute-start.4 = (f32[5,2,32,128]{3,2,1,0:T(8,128)S(1)}, f32[5,2,32,128]{3,2,1,0:T(8,128)S(1)}, u32[]{:S(2)}, u32[]{:S(2)}) collective-permute-start(f32[5,2,32,128]{3,2,1,0:T(8,128)S(1)} %get-tuple-element.36), channel_id=1, source_target_pairs={{0,4},{4,8},{8,12},{12,16},{16,20},{20,24},{24,28},{1,5},{5,9},{9,... | collective-permute-start | bytes 491528 | tf_op jit(solution)/shard_map/ppermute | solution.py:27
  41.0 11.5 %collective-permute-start.5 = (f32[5,2,32,128]{3,2,1,0:T(8,128)S(1)}, f32[5,2,32,128]{3,2,1,0:T(8,128)S(1)}, u32[]{:S(2)}, u32[]{:S(2)}) collective-permute-start(f32[5,2,32,128]{3,2,1,0:T(8,128)S(1)} %get-tuple-element.37), channel_id=1, source_target_pairs={{4,0},{8,4},{12,8},{16,12},{20,16},{24,20},{28,24},{5,1},{9,5},{13... | collective-permute-start | bytes 491528 | tf_op jit(solution)/shard_map/ppermute | solution.py:29
  42.4 173.1 %copy-start.13 = (s32[64]{0:T(128)}, s32[64]{0:T(128)S(1)}, u32[]{:S(2)}) copy-start(s32[64]{0:T(128)S(1)} %fusion.52) | copy-start | bytes 772
  44.1 179.2 %all-to-all-start.2 = ((bf16[32,1,4]{2,1,0:T(2,128)(2,1)}), bf16[32,1,4]{2,1,0:T(2,128)(2,1)S(1)}, u32[]{:S(2)}, u32[]{:S(2)}) async-start(bf16[32,1,4]{2,1,0:T(2,128)(2,1)} %all_to_all.16), calls=%async_computation.2 | async-start | bytes 32768 | tf_op jit(solution)/shard_map/all_to_all | solution.py:148
  52.6 6.6 %copy-start.4 = (f32[5,16,32,128]{3,2,1,0:T(8,128)S(1)}, f32[5,16,32,128]{3,2,1,0:T(8,128)}, u32[]{:S(2)}) copy-start(f32[5,16,32,128]{3,2,1,0:T(8,128)} %copy-done.3) | copy-start | bytes 3932164
  53.9 6.1 %collective-permute-start.6 = (f32[5,20,2,128]{3,2,1,0:T(2,128)S(1)}, f32[5,20,2,128]{3,2,1,0:T(2,128)S(1)}, u32[]{:S(2)}, u32[]{:S(2)}) collective-permute-start(f32[5,20,2,128]{3,2,1,0:T(2,128)S(1)} %get-tuple-element.30), channel_id=1, source_target_pairs={{0,1},{1,2},{2,3},{4,5},{5,6},{6,7},{8,9},{9,10},{10,11},{12,13},{... | collective-permute-start | bytes 307208 | tf_op jit(solution)/shard_map/ppermute | solution.py:27
  57.5 6.6 %collective-permute-start.7 = (f32[5,20,2,128]{3,2,1,0:T(2,128)S(1)}, f32[5,20,2,128]{3,2,1,0:T(2,128)S(1)}, u32[]{:S(2)}, u32[]{:S(2)}) collective-permute-start(f32[5,20,2,128]{3,2,1,0:T(2,128)S(1)} %get-tuple-element.31), channel_id=1, source_target_pairs={{1,0},{2,1},{3,2},{5,4},{6,5},{7,6},{9,8},{10,9},{11,10},{13,12},{... | collective-permute-start | bytes 307208 | tf_op jit(solution)/shard_map/ppermute | solution.py:29
  69.8 8.1 %copy-start.11 = (s32[2,4,16]{2,1,0:T(4,128)S(1)}, s32[2,4,16]{2,1,0:T(4,128)}, u32[]{:S(2)}) copy-start(s32[2,4,16]{2,1,0:T(4,128)} %param.11) | copy-start | bytes 1540
  73.7 1.1 copy-start.1
  74.8 83.0 %collective-permute-start.8 = (f32[5,2,32,128]{3,2,1,0:T(8,128)S(1)}, f32[5,2,32,128]{3,2,1,0:T(8,128)S(1)}, u32[]{:S(2)}, u32[]{:S(2)}) collective-permute-start(f32[5,2,32,128]{3,2,1,0:T(8,128)S(1)} %get-tuple-element.34), channel_id=1, source_target_pairs={{0,4},{4,8},{8,12},{12,16},{16,20},{20,24},{24,28},{1,5},{5,9},{9,... | collective-permute-start | bytes 491528 | tf_op jit(solution)/shard_map/ppermute | solution.py:27
  76.1 81.7 %collective-permute-start.9 = (f32[5,2,32,128]{3,2,1,0:T(8,128)S(1)}, f32[5,2,32,128]{3,2,1,0:T(8,128)S(1)}, u32[]{:S(2)}, u32[]{:S(2)}) collective-permute-start(f32[5,2,32,128]{3,2,1,0:T(8,128)S(1)} %get-tuple-element.35), channel_id=1, source_target_pairs={{4,0},{8,4},{12,8},{16,12},{20,16},{24,20},{28,24},{5,1},{9,5},{13... | collective-permute-start | bytes 491528 | tf_op jit(solution)/shard_map/ppermute | solution.py:29
  157.8 6.1 %copy-start.2 = (f32[5,16,32,128]{3,2,1,0:T(8,128)S(1)}, f32[5,16,32,128]{3,2,1,0:T(8,128)}, u32[]{:S(2)}) copy-start(f32[5,16,32,128]{3,2,1,0:T(8,128)} %copy-done.1) | copy-start | bytes 3932164
  159.1 5.6 %collective-permute-start.10 = (f32[5,20,2,128]{3,2,1,0:T(2,128)S(1)}, f32[5,20,2,128]{3,2,1,0:T(2,128)S(1)}, u32[]{:S(2)}, u32[]{:S(2)}) collective-permute-start(f32[5,20,2,128]{3,2,1,0:T(2,128)S(1)} %get-tuple-element.26), channel_id=1, source_target_pairs={{0,1},{1,2},{2,3},{4,5},{5,6},{6,7},{8,9},{9,10},{10,11},{12,13},{... | collective-permute-start | bytes 307208 | tf_op jit(solution)/shard_map/ppermute | solution.py:27
  162.5 6.6 %collective-permute-start.11 = (f32[5,20,2,128]{3,2,1,0:T(2,128)S(1)}, f32[5,20,2,128]{3,2,1,0:T(2,128)S(1)}, u32[]{:S(2)}, u32[]{:S(2)}) collective-permute-start(f32[5,20,2,128]{3,2,1,0:T(2,128)S(1)} %get-tuple-element.27), channel_id=1, source_target_pairs={{1,0},{2,1},{3,2},{5,4},{6,5},{7,6},{9,8},{10,9},{11,10},{13,12},{... | collective-permute-start | bytes 307208 | tf_op jit(solution)/shard_map/ppermute | solution.py:29
  223.3 19.0 %all-to-all-start.1 = ((bf16[32,4,2,512]{3,2,1,0:T(2,128)(2,1)}), bf16[32,4,2,512]{3,2,1,0:T(2,128)(2,1)S(1)}, u32[]{:S(2)}, u32[]{:S(2)}) async-start(bf16[32,4,2,512]{3,2,1,0:T(2,128)(2,1)} %bitcast.11), calls=%async_computation.1 | async-start | bytes 524288 | tf_op jit(solution)/shard_map/all_to_all | solution.py:147
  242.2 36.4 %all-to-all-start = ((bf16[32,4,2,2560]{3,2,1,0:T(2,128)(2,1)}), bf16[32,4,2,2560]{3,2,1,0:T(2,128)(2,1)}, u32[]{:S(2)}, u32[]{:S(2)}) async-start(bf16[32,4,2,2560]{3,2,1,0:T(2,128)(2,1)} %bitcast.72), calls=%async_computation | async-start | bytes 2621440 | tf_op jit(solution)/shard_map/all_to_all | solution.py:146
  248.3 197.1 %all-reduce.5.cloned.1.call-start = ((), (), s32[]{:S(2)}) async-start(), calls=%async_computation.3 | async-start | bytes 10485760 | tf_op jit(solution)/shard_map/psum | solution.py:159
  282.7 2.3 copy-start.5
  282.7 2.3 copy-start.10
  285.1 1.0 copy-start.9
  285.1 1.8 copy-start.14
  285.1 1.8 copy-start.15
  285.8 2.4 copy-start.7
  297.2 4.1 copy-start.8
Sparse Core Ops, SparseCore 0:
  297.3 148.0 all-reduce.4
where the time goes:
time: 466 us; the launch traced here: 458 us
  waiting for transfers between devices  185 us (40%)
  local copies, waits for them, and re-layouts  154 us (33%)
  starting transfers between devices  48.8 us (10%)
  other arithmetic  34.4 us (7%)
  matrix products  20.8 us (4%)
  between operations  14.9 us (3%)
    psum x1, waiting for transfers between devices, per_device(): patch_gradient = lax.psum(partial_value, ('gx', 'gy'))  141 us
    reshape x3, local copies, waits for them, and re-layouts, patchify(): state.reshape(FIELDS, width_x // PATCH, PATCH, width_y // PATCH, PATCH, w...  43.3 us
    reshape x3, local copies, waits for them, and re-layouts, patchify(): shaped.transpose(1, 3, 5, 0, 2, 4, 6).reshape(-1, FIELDS * PATCH ** 3)  36.3 us
    transpose x3, local copies, waits for them, and re-layouts, patchify(): shaped.transpose(1, 3, 5, 0, 2, 4, 6).reshape(-1, FIELDS * PATCH ** 3)  34.6 us
    all_to_all x1, waiting for transfers between devices, per_device(): lax.all_to_all(into_slots(picked), ('gx', 'gy'), split_axis=0, concat_axi...  29 us
    ppermute x6, starting transfers between devices, with_halo(): lax.ppermute(tail, axis, [(i, (i + 1) % count) for i in range(ends)])  18.6 us
    scatter x2, local copies, waits for them, and re-layouts, into_slots(): buffer = jnp.zeros((devices * slot_count, BLOCK_ROWS, width), rows.dtype)...  16 us
    ppermute x6, waiting for transfers between devices, with_halo(): lax.ppermute(head, axis, [((i + 1) % count, i) for i in range(ends)])  13.3 us
  transfers between devices with their start and end apart: 16, of which 9 were waited for; matrix products, arithmetic and copies ran while one was open for 37% of the time, Pallas kernels for 0%

commit v1 on v0

--- a/solution.py
+++ b/solution.py
@@ -156,7 +156,7 @@
         source, got_target.reshape(-1, EMBED), valid_rows, w_in[0], b_in[0], w_out[0], b_out[0]
     )
     partial_value = contract_rows(flat_patches, results[0])
-    patch_gradient = lax.psum(partial_value, ("gx", "gy"))
+    patch_gradient = lax.psum(lax.psum(partial_value, "gx"), "gy")
     return (
         states[-1],
         patch_gradient,

time: 466 us -> 601 us (1.29)
  waiting for transfers between devices: 185 us -> 321 us
    psum x1 -> x2, waiting for transfers between devices: 141 us -> 277 us  [per_device(): patch_gradient = lax.psum(lax.psum(partial_value, 'gx'), 'gy')]
  transfers between devices with their start and end apart: 16 -> 17, of which waited for: 9 -> 10; matrix products, arithmetic and copies ran while one was open for 37% -> 29% of each run, Pallas kernels for 0% -> 0%
where the time goes in v1:
time: 601 us; the launch traced here: 594 us
  waiting for transfers between devices  321 us (53%)
  local copies, waits for them, and re-layouts  154 us (26%)
  starting transfers between devices  48.8 us (8%)
  other arithmetic  34.4 us (6%)
  matrix products  20.8 us (3%)
  between operations  14.9 us (2%)
    psum x2, waiting for transfers between devices, per_device(): patch_gradient = lax.psum(lax.psum(partial_value, 'gx'), 'gy')  277 us
    reshape x3, local copies, waits for them, and re-layouts, patchify(): state.reshape(FIELDS, width_x // PATCH, PATCH, width_y // PATCH, PATCH, w...  43.3 us
    reshape x3, local copies, waits for them, and re-layouts, patchify(): shaped.transpose(1, 3, 5, 0, 2, 4, 6).reshape(-1, FIELDS * PATCH ** 3)  36.3 us
    transpose x3, local copies, waits for them, and re-layouts, patchify(): shaped.transpose(1, 3, 5, 0, 2, 4, 6).reshape(-1, FIELDS * PATCH ** 3)  34.6 us
    all_to_all x1, waiting for transfers between devices, per_device(): lax.all_to_all(into_slots(picked), ('gx', 'gy'), split_axis=0, concat_axi...  29 us
    ppermute x6, starting transfers between devices, with_halo(): lax.ppermute(tail, axis, [(i, (i + 1) % count) for i in range(ends)])  18.6 us
    scatter x2, local copies, waits for them, and re-layouts, into_slots(): buffer = jnp.zeros((devices * slot_count, BLOCK_ROWS, width), rows.dtype)...  16 us
    ppermute x6, waiting for transfers between devices, with_halo(): lax.ppermute(head, axis, [((i + 1) % count, i) for i in range(ends)])  13.3 us
  transfers between devices with their start and end apart: 17, of which 10 were waited for; matrix products, arithmetic and copies ran while one was open for 29% of the time, Pallas kernels for 0%

profile of v1, /device:TPU:0, one launch (start us, length us, event | category | flops | bytes accessed | tf_op | source)
XLA Modules:
  0.0 593.6 jit_solution(2547997327838988676)
XLA Ops:
  8.4 2.4 collective-permute-start
  10.8 1.3 collective-permute-start.1
  13.8 1.8 constant_dynamic-update-slice_fusion
  16.3 3.8 collective-permute-start.2
  22.3 4.3 collective-permute-done.3
  26.6 1.6 select_maximum_fusion.8
  28.2 2.3 broadcast_multiply_fusion.2
  31.9 4.0 fusion.57
  37.0 4.0 collective-permute-start.4
  44.1 8.5 %all-to-all-start.2 = ((bf16[32,1,4]{2,1,0:T(2,128)(2,1)}), bf16[32,1,4]{2,1,0:T(2,128)(2,1)S(1)}, u32[]{:S(2)}, u32[]{:S(2)}) async-start(bf16[32,1,4]{2,1,0:T(2,128)(2,1)} %all_to_all.16), calls=%async_computation.2 | async-start | bytes 32768 | tf_op jit(solution)/shard_map/all_to_all | solution.py:148
  53.9 3.7 collective-permute-start.6
  57.5 1.6 collective-permute-start.7
  59.9 4.2 collective-permute-done.7
  64.1 3.5 select_maximum_fusion.4
  69.8 3.9 fusion.59
  74.8 1.3 collective-permute-start.8
  76.1 1.8 collective-permute-start.9
  78.6 14.4 %reshape.78 = bf16[5,2,8,4,8,16,8]{6,5,4,3,2,1,0:T(8,128)(2,1)} reshape(bf16[5,16,32,128]{3,2,1,0:T(8,128)(2,1)} %get-tuple-element.8) | data formatting | bytes 1310720 | tf_op jit(solution)/shard_map/reshape | solution.py:96
  93.1 10.7 %copy.18 = bf16[2,4,16,5,8,8,8]{6,5,4,3,2,1,0:T(8,128)(2,1)} copy(bf16[2,4,16,5,8,8,8]{6,2,5,1,4,0,3:T(8,128)(2,1)} %bitcast.69) | data formatting | bytes 1310720 | tf_op jit(solution)/shard_map/transpose | solution.py:99
  103.8 14.5 %reshape.79 = bf16[64,2,2560]{2,1,0:T(2,128)(2,1)} reshape(bf16[2,4,16,5,8,8,8]{6,5,4,3,2,1,0:T(8,128)(2,1)} %copy.18) | data formatting | bytes 1310720 | tf_op jit(solution)/shard_map/reshape | solution.py:99
  118.3 14.4 %reshape.76 = bf16[5,2,8,4,8,16,8]{6,5,4,3,2,1,0:T(8,128)(2,1)} reshape(bf16[5,16,32,128]{3,2,1,0:T(8,128)(2,1)} %get-tuple-element.10) | data formatting | bytes 1310720 | tf_op jit(solution)/shard_map/reshape | solution.py:96
  132.7 10.6 %copy.17 = bf16[2,4,16,5,8,8,8]{6,5,4,3,2,1,0:T(8,128)(2,1)} copy(bf16[2,4,16,5,8,8,8]{6,2,5,1,4,0,3:T(8,128)(2,1)} %bitcast.70) | data formatting | bytes 1310720 | tf_op jit(solution)/shard_map/transpose | solution.py:99
  143.3 14.5 %reshape.77 = bf16[64,2,2560]{2,1,0:T(2,128)(2,1)} reshape(bf16[2,4,16,5,8,8,8]{6,5,4,3,2,1,0:T(8,128)(2,1)} %copy.17) | data formatting | bytes 1310720 | tf_op jit(solution)/shard_map/reshape | solution.py:99
  159.1 3.4 collective-permute-start.10
  162.5 1.5 collective-permute-start.11
  164.7 4.3 collective-permute-done.11
  169.0 3.5 select_maximum_fusion
  174.8 4.1 fusion.55
  178.9 14.4 %reshape.82 = bf16[5,2,8,4,8,16,8]{6,5,4,3,2,1,0:T(8,128)(2,1)} reshape(bf16[5,16,32,128]{3,2,1,0:T(8,128)(2,1)} %get-tuple-element.6) | data formatting | bytes 1310720 | tf_op jit(solution)/shard_map/reshape | solution.py:96
  193.3 13.3 %copy.19 = bf16[2,4,16,5,8,8,8]{2,1,0,6,5,4,3:T(4,128)(2,1)} copy(bf16[2,4,16,5,8,8,8]{6,2,5,1,4,0,3:T(8,128)(2,1)} %bitcast.71) | data formatting | bytes 1310720 | tf_op jit(solution)/shard_map/transpose | solution.py:99
  206.6 7.3 %reshape.83 = bf16[128,2560]{0,1:T(8,128)(2,1)S(1)} reshape(bf16[2,4,16,5,8,8,8]{2,1,0,6,5,4,3:T(4,128)(2,1)} %copy.19) | data formatting | bytes 1310720 | tf_op jit(solution)/shard_map/reshape | solution.py:99
  215.4 7.8 %scatter_fusion.1 = bf16[128,2,512]{2,1,0:T(2,128)(2,1)} fusion(bf16[128,2,512]{2,1,0:T(2,128)(2,1)} %broadcast_in_dim.41, s32[64]{0:T(128)S(1)} %fusion.52, bf16[64,2,512]{2,1,0:T(2,128)(2,1)S(1)} %reshape.99), kind=kCustom, calls=%fused_computation.1 | custom fusion | bytes 393472 | tf_op jit(solution)/shard_map/scatter | solution.py:139
  223.3 6.9 %all-to-all-start.1 = ((bf16[32,4,2,512]{3,2,1,0:T(2,128)(2,1)}), bf16[32,4,2,512]{3,2,1,0:T(2,128)(2,1)S(1)}, u32[]{:S(2)}, u32[]{:S(2)}) async-start(bf16[32,4,2,512]{3,2,1,0:T(2,128)(2,1)} %bitcast.11), calls=%async_computation.1 | async-start | bytes 524288 | tf_op jit(solution)/shard_map/all_to_all | solution.py:147
  230.2 2.1 broadcast_select_fusion
  232.3 1.7 broadcast_in_dim.39
  234.0 8.2 %scatter_fusion = bf16[128,2,2560]{2,1,0:T(2,128)(2,1)} fusion(bf16[128,2,2560]{2,1,0:T(2,128)(2,1)} %broadcast_in_dim.39, s32[64]{0:T(128)} %copy-done.13, bf16[64,2,2560]{2,1,0:T(2,128)(2,1)S(1)} %broadcast_select_fusion), kind=kCustom, calls=%fused_computation | custom fusion | bytes 1966336 | tf_op jit(solution)/shard_map/scatter | solution.py:139
  242.2 6.1 %all-to-all-start = ((bf16[32,4,2,2560]{3,2,1,0:T(2,128)(2,1)}), bf16[32,4,2,2560]{3,2,1,0:T(2,128)(2,1)}, u32[]{:S(2)}, u32[]{:S(2)}) async-start(bf16[32,4,2,2560]{3,2,1,0:T(2,128)(2,1)} %bitcast.72), calls=%async_computation | async-start | bytes 2621440 | tf_op jit(solution)/shard_map/all_to_all | solution.py:146
  249.6 29.0 %all-to-all-done = bf16[32,4,2,2560]{3,2,1,0:T(2,128)(2,1)} async-done(((bf16[32,4,2,2560]{3,2,1,0:T(2,128)(2,1)}), bf16[32,4,2,2560]{3,2,1,0:T(2,128)(2,1)}, u32[]{:S(2)}, u32[]{:S(2)}) %all-to-all-start) | async-done | bytes 1310752 | tf_op jit(solution)/shard_map/all_to_all | solution.py:146
  278.7 4.1 reshape.81
  282.7 2.3 convolution_convert_fusion
  286.9 1.3 convert_reduce_fusion.1
  288.2 2.7 convert_reduce_fusion
  290.9 6.2 %fusion.46 = f32[2560,512]{1,0:T(8,128)} fusion(bf16[256,2560]{1,0:T(8,128)(2,1)} %reshape.81, bf16[256,2048]{1,0:T(8,128)(2,1)} %get-tuple-element.48, bf16[1,512,2048]{2,1,0:T(8,128)(2,1)} %param.12), kind=kOutput, calls=%fused_computation.96 | convolution fusion | flops 1208090624 | bytes 9699328 | tf_op jit(solution)/shard_map/dot_general | solution.py:67
  297.2 92.5 %all-reduce.6.cloned.1.call-done = f32[2560,512]{1,0:T(8,128)} async-done(((f32[2560,512]{1,0:T(8,128)}), f32[2560,512]{1,0:T(8,128)}) %all-reduce.6.cloned.1.call-update) | async-done | bytes 5242896 | tf_op jit(solution)/shard_map/psum | solution.py:159
  389.8 4.1 convolution_bitcast_fusion.1
  393.9 2.8 convolution_bitcast_fusion
  396.8 184.4 %all-reduce.8.cloned.1.call-done = f32[2560,512]{1,0:T(8,128)} async-done(((f32[2560,512]{1,0:T(8,128)}), f32[2560,512]{1,0:T(8,128)}) %all-reduce.8.cloned.1.call-update) | async-done | bytes 5242896 | tf_op jit(solution)/shard_map/psum | solution.py:159
  581.2 5.4 copy.41
  (99 shorter events, 25.9 us)
Async XLA Ops:
  7.2 206.8 %copy-start = (bf16[2560,512]{1,0:T(8,128)(2,1)S(1)}, bf16[2560,512]{1,0:T(8,128)(2,1)}, u32[]{:S(2)}) copy-start(bf16[2560,512]{1,0:T(8,128)(2,1)} %param.9) | copy-start | bytes 7864324
  8.4 5.4 collective-permute-start
  10.8 5.4 collective-permute-start.1
  16.3 6.0 %collective-permute-start.2 = (f32[5,20,2,128]{3,2,1,0:T(2,128)S(1)}, f32[5,20,2,128]{3,2,1,0:T(2,128)S(1)}, u32[]{:S(2)}, u32[]{:S(2)}) collective-permute-start(f32[5,20,2,128]{3,2,1,0:T(2,128)S(1)} %get-tuple-element.32), channel_id=1, source_target_pairs={{0,1},{1,2},{2,3},{4,5},{5,6},{6,7},{8,9},{9,10},{10,11},{12,13},{... | collective-permute-start | bytes 307208 | tf_op jit(solution)/shard_map/ppermute | solution.py:27
  20.1 6.6 %collective-permute-start.3 = (f32[5,20,2,128]{3,2,1,0:T(2,128)S(1)}, f32[5,20,2,128]{3,2,1,0:T(2,128)S(1)}, u32[]{:S(2)}, u32[]{:S(2)}) collective-permute-start(f32[5,20,2,128]{3,2,1,0:T(2,128)S(1)} %get-tuple-element.33), channel_id=1, source_target_pairs={{1,0},{2,1},{3,2},{5,4},{6,5},{7,6},{9,8},{10,9},{11,10},{13,12},{... | collective-permute-start | bytes 307208 | tf_op jit(solution)/shard_map/ppermute | solution.py:29
  30.6 1.3 copy-start.6
  31.9 10.4 %copy-start.12 = (s32[64,1]{0,1:T(1,128)S(1)}, s32[64,1]{0,1:T(1,128)}, u32[]{:S(2)}) copy-start(s32[64,1]{0,1:T(1,128)} %param.10) | copy-start | bytes 772
  35.9 1.1 copy-start.3
  37.0 15.6 %collective-permute-start.4 = (f32[5,2,32,128]{3,2,1,0:T(8,128)S(1)}, f32[5,2,32,128]{3,2,1,0:T(8,128)S(1)}, u32[]{:S(2)}, u32[]{:S(2)}) collective-permute-start(f32[5,2,32,128]{3,2,1,0:T(8,128)S(1)} %get-tuple-element.36), channel_id=1, source_target_pairs={{0,4},{4,8},{8,12},{12,16},{16,20},{20,24},{24,28},{1,5},{5,9},{9,... | collective-permute-start | bytes 491528 | tf_op jit(solution)/shard_map/ppermute | solution.py:27
  41.0 11.5 %collective-permute-start.5 = (f32[5,2,32,128]{3,2,1,0:T(8,128)S(1)}, f32[5,2,32,128]{3,2,1,0:T(8,128)S(1)}, u32[]{:S(2)}, u32[]{:S(2)}) collective-permute-start(f32[5,2,32,128]{3,2,1,0:T(8,128)S(1)} %get-tuple-element.37), channel_id=1, source_target_pairs={{4,0},{8,4},{12,8},{16,12},{20,16},{24,20},{28,24},{5,1},{9,5},{13... | collective-permute-start | bytes 491528 | tf_op jit(solution)/shard_map/ppermute | solution.py:29
  42.4 173.1 %copy-start.13 = (s32[64]{0:T(128)}, s32[64]{0:T(128)S(1)}, u32[]{:S(2)}) copy-start(s32[64]{0:T(128)S(1)} %fusion.52) | copy-start | bytes 772
  44.1 179.2 %all-to-all-start.2 = ((bf16[32,1,4]{2,1,0:T(2,128)(2,1)}), bf16[32,1,4]{2,1,0:T(2,128)(2,1)S(1)}, u32[]{:S(2)}, u32[]{:S(2)}) async-start(bf16[32,1,4]{2,1,0:T(2,128)(2,1)} %all_to_all.16), calls=%async_computation.2 | async-start | bytes 32768 | tf_op jit(solution)/shard_map/all_to_all | solution.py:148
  52.6 6.6 %copy-start.4 = (f32[5,16,32,128]{3,2,1,0:T(8,128)S(1)}, f32[5,16,32,128]{3,2,1,0:T(8,128)}, u32[]{:S(2)}) copy-start(f32[5,16,32,128]{3,2,1,0:T(8,128)} %copy-done.3) | copy-start | bytes 3932164
  53.9 6.1 %collective-permute-start.6 = (f32[5,20,2,128]{3,2,1,0:T(2,128)S(1)}, f32[5,20,2,128]{3,2,1,0:T(2,128)S(1)}, u32[]{:S(2)}, u32[]{:S(2)}) collective-permute-start(f32[5,20,2,128]{3,2,1,0:T(2,128)S(1)} %get-tuple-element.30), channel_id=1, source_target_pairs={{0,1},{1,2},{2,3},{4,5},{5,6},{6,7},{8,9},{9,10},{10,11},{12,13},{... | collective-permute-start | bytes 307208 | tf_op jit(solution)/shard_map/ppermute | solution.py:27
  57.5 6.6 %collective-permute-start.7 = (f32[5,20,2,128]{3,2,1,0:T(2,128)S(1)}, f32[5,20,2,128]{3,2,1,0:T(2,128)S(1)}, u32[]{:S(2)}, u32[]{:S(2)}) collective-permute-start(f32[5,20,2,128]{3,2,1,0:T(2,128)S(1)} %get-tuple-element.31), channel_id=1, source_target_pairs={{1,0},{2,1},{3,2},{5,4},{6,5},{7,6},{9,8},{10,9},{11,10},{13,12},{... | collective-permute-start | bytes 307208 | tf_op jit(solution)/shard_map/ppermute | solution.py:29
  69.8 8.1 %copy-start.11 = (s32[2,4,16]{2,1,0:T(4,128)S(1)}, s32[2,4,16]{2,1,0:T(4,128)}, u32[]{:S(2)}) copy-start(s32[2,4,16]{2,1,0:T(4,128)} %param.11) | copy-start | bytes 1540
  73.7 1.1 copy-start.1
  74.8 83.0 %collective-permute-start.8 = (f32[5,2,32,128]{3,2,1,0:T(8,128)S(1)}, f32[5,2,32,128]{3,2,1,0:T(8,128)S(1)}, u32[]{:S(2)}, u32[]{:S(2)}) collective-permute-start(f32[5,2,32,128]{3,2,1,0:T(8,128)S(1)} %get-tuple-element.34), channel_id=1, source_target_pairs={{0,4},{4,8},{8,12},{12,16},{16,20},{20,24},{24,28},{1,5},{5,9},{9,... | collective-permute-start | bytes 491528 | tf_op jit(solution)/shard_map/ppermute | solution.py:27
  76.1 81.7 %collective-permute-start.9 = (f32[5,2,32,128]{3,2,1,0:T(8,128)S(1)}, f32[5,2,32,128]{3,2,1,0:T(8,128)S(1)}, u32[]{:S(2)}, u32[]{:S(2)}) collective-permute-start(f32[5,2,32,128]{3,2,1,0:T(8,128)S(1)} %get-tuple-element.35), channel_id=1, source_target_pairs={{4,0},{8,4},{12,8},{16,12},{20,16},{24,20},{28,24},{5,1},{9,5},{13... | collective-permute-start | bytes 491528 | tf_op jit(solution)/shard_map/ppermute | solution.py:29
  157.8 6.1 %copy-start.2 = (f32[5,16,32,128]{3,2,1,0:T(8,128)S(1)}, f32[5,16,32,128]{3,2,1,0:T(8,128)}, u32[]{:S(2)}) copy-start(f32[5,16,32,128]{3,2,1,0:T(8,128)} %copy-done.1) | copy-start | bytes 3932164
  159.1 5.6 collective-permute-start.10
  162.5 6.6 %collective-permute-start.11 = (f32[5,20,2,128]{3,2,1,0:T(2,128)S(1)}, f32[5,20,2,128]{3,2,1,0:T(2,128)S(1)}, u32[]{:S(2)}, u32[]{:S(2)}) collective-permute-start(f32[5,20,2,128]{3,2,1,0:T(2,128)S(1)} %get-tuple-element.27), channel_id=1, source_target_pairs={{1,0},{2,1},{3,2},{5,4},{6,5},{7,6},{9,8},{10,9},{11,10},{13,12},{... | collective-permute-start | bytes 307208 | tf_op jit(solution)/shard_map/ppermute | solution.py:29
  223.3 19.0 %all-to-all-start.1 = ((bf16[32,4,2,512]{3,2,1,0:T(2,128)(2,1)}), bf16[32,4,2,512]{3,2,1,0:T(2,128)(2,1)S(1)}, u32[]{:S(2)}, u32[]{:S(2)}) async-start(bf16[32,4,2,512]{3,2,1,0:T(2,128)(2,1)} %bitcast.11), calls=%async_computation.1 | async-start | bytes 524288 | tf_op jit(solution)/shard_map/all_to_all | solution.py:147
  242.2 36.4 %all-to-all-start = ((bf16[32,4,2,2560]{3,2,1,0:T(2,128)(2,1)}), bf16[32,4,2,2560]{3,2,1,0:T(2,128)(2,1)}, u32[]{:S(2)}, u32[]{:S(2)}) async-start(bf16[32,4,2,2560]{3,2,1,0:T(2,128)(2,1)} %bitcast.72), calls=%async_computation | async-start | bytes 2621440 | tf_op jit(solution)/shard_map/all_to_all | solution.py:146
  248.3 141.5 %all-reduce.6.cloned.1.call-start = ((), (), s32[]{:S(2)}) async-start(), calls=%async_computation.3 | async-start | bytes 10485760 | tf_op jit(solution)/shard_map/psum | solution.py:159
  282.7 2.3 copy-start.5
  282.7 2.3 copy-start.10
  285.1 1.0 copy-start.9
  285.1 1.8 copy-start.14
  285.1 1.8 copy-start.15
  285.8 2.4 copy-start.7
  297.2 284.0 %all-reduce.8.cloned.1.call-start = ((), (), s32[]{:S(2)}) async-start(), calls=%async_computation.4 | async-start | bytes 10485760 | tf_op jit(solution)/shard_map/psum | solution.py:159
  389.8 4.1 copy-start.8
Sparse Core Ops, SparseCore 0:
  297.3 92.3 all-reduce.5
  392.1 188.9 all-reduce.7
